TPU v7x, 128 devices: a whole 4x4x4 slice. The times are simulated.
128 devices in a mesh: grp: 16 (over z, y), mem: 8 (over x, core).
Axes of the slice: x: 4, y: 4, z: 4, core: 2. Of those that a mesh axis runs over, the one named last changes fastest.
Arguments:
- queries: bfloat16 [32768, 2048], P(('grp', 'mem')), may hold values from -6 to 6
- keys: bfloat16 [32768, 2048], P(('grp', 'mem')), may hold values from -6 to 6
- values: bfloat16 [32768, 2048], P(('grp', 'mem')), may hold values from -6 to 6
- grad_out: bfloat16 [32768, 2048], P(('grp', 'mem')), may hold values from -0.0625 to 0.0625
- log_decay: float32 [8, 32768], P(None, ('grp', 'mem')), may hold values from -1.6 to 0
Outputs:
- grad_queries: bfloat16 [32768, 2048], P(('grp', 'mem'))
- grad_keys: bfloat16 [32768, 2048], P(('grp', 'mem'))
- grad_values: bfloat16 [32768, 2048], P(('grp', 'mem'))
All inputs are finite; a program needn't handle non-finite values.
Results may differ from a plain program's by a relative error of at most 0.0052.
Values sent between devices are 32-bit elements; how exact they have to be, the bound alone decides.
A program may use at most 128 MiB of HBM per device.

v0:
```python
import jax
import jax.numpy as jnp
from jax import lax
from jax.sharding import Mesh
from jax.sharding import PartitionSpec as P

HEAD_COUNT = 8
DK = 256
DV = 256
BLOCK = 128
GRP = ("grp_0", "grp_1")
GRP_MEM = ("grp_0", "grp_1", "mem")


def filled_with(x, identity):
    return jax.tree.map(
        lambda part, zero: jnp.zeros_like(part) + jnp.asarray(zero, part.dtype), x, identity
    )


def entering(x, axes, combine, identity, reverse):
    before = start = filled_with(x, identity)
    total = x
    for axis in reversed(axes):
        length, mine = (lax.axis_size(axis), lax.axis_index(axis))
        pieces = jax.tree.map(lambda part: lax.all_gather(part, axis), total)
        inside, total = (start, start)
        for k in reversed(range(length)) if reverse else range(length):
            passed = k > mine if reverse else k < mine
            total = combine(total, jax.tree.map(lambda part: part[k], pieces))
            inside = jax.tree.map(lambda new, old: jnp.where(passed, new, old), total, inside)
        before = combine(inside, before)
    return before


def chain(earlier, later):
    early_decay, early_state = earlier
    late_decay, late_state = later
    return (early_decay * late_decay, late_state + late_decay[:, None, None] * early_state)


def body(queries, keys, values, grad_out, log_decay):
    tokens = queries.shape[0]
    count = tokens // BLOCK
    scale = DK ** (-0.5)
    query_blocks = queries.reshape(count, BLOCK, HEAD_COUNT, DK)
    key_blocks = keys.reshape(count, BLOCK, HEAD_COUNT, DK)
    value_blocks = values.reshape(count, BLOCK, HEAD_COUNT, DV)
    grad_blocks = grad_out.reshape(count, BLOCK, HEAD_COUNT, DV)
    logs = jnp.transpose(log_decay.reshape(HEAD_COUNT, count, BLOCK), (1, 0, 2))
    cumul = jnp.cumsum(logs, axis=2)
    ends = cumul[:, :, -1]
    lower = jnp.tril(jnp.ones((BLOCK, BLOCK), dtype=bool))
    spread = cumul[:, :, :, None] - cumul[:, :, None, :]
    decay = jnp.where(lower, jnp.exp(jnp.where(lower, spread, 0.0)), 0.0)
    scores = jnp.einsum(
        "bthe,bshe->bhts", grad_blocks, value_blocks, preferred_element_type=jnp.float32
    )
    weight_grad = (scores * decay).astype(jnp.bfloat16)
    attend = jnp.einsum(
        "bthd,bshd->bhts", query_blocks, key_blocks, preferred_element_type=jnp.float32
    )
    weight_value = (attend * decay).astype(jnp.bfloat16)
    inner_query = jnp.einsum(
        "bhts,bshd->bthd", weight_grad, key_blocks, preferred_element_type=jnp.float32
    )
    inner_key = jnp.einsum(
        "bhts,bthd->bshd", weight_grad, query_blocks, preferred_element_type=jnp.float32
    )
    inner_value = jnp.einsum(
        "bhts,bthe->bshe", weight_value, grad_blocks, preferred_element_type=jnp.float32
    )
    head_factor = jnp.exp(jnp.transpose(cumul, (0, 2, 1)))[..., None]
    tail_factor = jnp.exp(jnp.transpose(ends[:, :, None] - cumul, (0, 2, 1)))[..., None]
    keys_decayed = (key_blocks * tail_factor).astype(jnp.bfloat16)
    queries_decayed = (query_blocks * head_factor).astype(jnp.bfloat16)
    forward_parts = jnp.einsum(
        "bshd,bshe->bhde", keys_decayed, value_blocks, preferred_element_type=jnp.float32
    )
    reverse_parts = jnp.einsum(
        "bthd,bthe->bhde", queries_decayed, grad_blocks, preferred_element_type=jnp.float32
    )
    block_decay = jnp.exp(ends)
    running = jnp.zeros((HEAD_COUNT, DK, DV), jnp.float32)
    carried = jnp.ones((HEAD_COUNT,), jnp.float32)
    prefix_list = []
    carried_list = []
    for position in range(count):
        prefix_list.append(running)
        carried_list.append(carried)
        running = block_decay[position][:, None, None] * running + forward_parts[position]
        carried = carried * block_decay[position]
    forward_total = running
    running = jnp.zeros((HEAD_COUNT, DK, DV), jnp.float32)
    after = jnp.ones((HEAD_COUNT,), jnp.float32)
    suffix_list = [None] * count
    after_list = [None] * count
    for position in reversed(range(count)):
        suffix_list[position] = running
        after_list[position] = after
        running = block_decay[position][:, None, None] * running + reverse_parts[position]
        after = after * block_decay[position]
    members = lax.axis_size("mem")
    decay_cols = jnp.broadcast_to(carried[None, :, None, None], (1, HEAD_COUNT, members, 1))
    pieces = (
        lax.all_to_all(decay_cols, "mem", split_axis=2, concat_axis=0, tiled=True),
        lax.all_to_all(forward_total[None], "mem", split_axis=2, concat_axis=0, tiled=True),
        lax.all_to_all(running[None], "mem", split_axis=2, concat_axis=0, tiled=True),
    )
    member_decays = pieces[0][:, :, 0, 0]
    width = DK // members
    share_identity = (
        jnp.ones((HEAD_COUNT,), jnp.float32),
        jnp.zeros((HEAD_COUNT, width, DV), jnp.float32),
    )
    forward_prefix = []
    accum = share_identity
    for index in range(members):
        forward_prefix.append(accum)
        accum = chain(accum, (member_decays[index], pieces[1][index]))
    forward_whole = accum
    reverse_prefix = [None] * members
    accum = share_identity
    for index in reversed(range(members)):
        reverse_prefix[index] = accum
        accum = chain(accum, (member_decays[index], pieces[2][index]))
    group_first = entering(forward_whole, GRP, chain, share_identity, False)
    group_second = entering(accum, GRP, chain, share_identity, True)
    first_stack = jnp.stack(
        [chain(group_first, forward_prefix[index])[1] for index in range(members)]
    )
    second_stack = jnp.stack(
        [chain(group_second, reverse_prefix[index])[1] for index in range(members)]
    )
    returned = (
        lax.all_to_all(first_stack, "mem", split_axis=0, concat_axis=2, tiled=True),
        lax.all_to_all(second_stack, "mem", split_axis=0, concat_axis=2, tiled=True),
    )
    state_from = returned[0][0]
    grads_from = returned[1][0]
    states_low = (
        jnp.stack(prefix_list) + jnp.stack(carried_list)[:, :, None, None] * state_from[None]
    ).astype(jnp.bfloat16)
    grads_low = (
        jnp.stack(suffix_list) + jnp.stack(after_list)[:, :, None, None] * grads_from[None]
    ).astype(jnp.bfloat16)
    outer_query = jnp.einsum(
        "bthe,bhde->bthd", grad_blocks, states_low, preferred_element_type=jnp.float32
    )
    outer_key = jnp.einsum(
        "bshe,bhde->bshd", value_blocks, grads_low, preferred_element_type=jnp.float32
    )
    outer_value = jnp.einsum(
        "bshd,bhde->bshe", key_blocks, grads_low, preferred_element_type=jnp.float32
    )
    grad_queries = (scale * (inner_query + head_factor * outer_query)).astype(jnp.bfloat16)
    grad_keys = (scale * (inner_key + tail_factor * outer_key)).astype(jnp.bfloat16)
    grad_values = (scale * (inner_value + tail_factor * outer_value)).astype(jnp.bfloat16)
    return (
        grad_queries.reshape(tokens, HEAD_COUNT * DK),
        grad_keys.reshape(tokens, HEAD_COUNT * DK),
        grad_values.reshape(tokens, HEAD_COUNT * DV),
    )


def solution(mesh):
    torus = Mesh(mesh.devices.reshape(4, 4, mesh.shape["mem"]), ("grp_0", "grp_1", "mem"))
    return jax.shard_map(
        body,
        mesh=torus,
        in_specs=(
            P(GRP_MEM, None),
            P(GRP_MEM, None),
            P(GRP_MEM, None),
            P(GRP_MEM, None),
            P(None, GRP_MEM),
        ),
        out_specs=(P(GRP_MEM, None), P(GRP_MEM, None), P(GRP_MEM, None)),
        check_vma=False,
    )
```

profile of v0, /device:TPU:1, one launch (start us, length us, event | category | flops | bytes accessed | tf_op | source)
XLA Modules:
  0.0 245.2 jit_solution(16652471330811321693)
XLA Ops:
  9.3 5.8 %all-to-all-start.1 = ((f32[1,8,8,1]{1,3,0,2:T(1,128)}), f32[1,8,8,1]{1,3,0,2:T(1,128)S(1)}, u32[]{:S(2)}, u32[]{:S(2)}) async-start(f32[1,8,8,1]{1,3,0,2:T(1,128)} %broadcast_in_dim.20), calls=%async_computation.1 | async-start | bytes 8192 | tf_op jit(solution)/shard_map/all_to_all | solution.py:106
  22.4 2.9 %slice_add_fusion = (f32[1,8,256,256]{3,2,1,0:T(8,128)S(1)}, f32[1,8,256,256]{3,2,1,0:T(8,128)S(1)}, f32[1,8,256,256]{3,2,1,0:T(8,128)}, f32[1,8,256,256]{3,2,1,0:T(8,128)}) fusion(f32[2,8,256,256]{3,2,1,0:T(8,128)S(1)} %fusion.15, f32[8]{0:T(128)S(1)} %get-tuple-element.70, f32[8]{0:T(128)S(1)} %get-tuple-element.73, f32[2,8,256,256]{3,2,1,0:T(8,128)S(1)} %fusion.14, ...), kind=kLoop, calls=%fused_computation.3 | loop fusion | flops 3145728 | bytes 16777344 | tf_op jit(solution)/shard_map/add | solution.py:101
  25.2 2.6 %copy.204 = f32[1,8,256,256]{3,1,0,2:T(8,128)} copy(f32[1,8,256,256]{3,2,1,0:T(8,128)S(1)} %get-tuple-element.23) | data formatting | bytes 4194304 | tf_op jit(solution)/shard_map/add | solution.py:101
  27.8 4.8 %all-to-all-start.3 = ((f32[1,8,256,256]{3,1,0,2:T(8,128)}), f32[1,8,256,256]{3,1,0,2:T(8,128)}, u32[]{:S(2)}, u32[]{:S(2)}) async-start(f32[1,8,256,256]{3,1,0,2:T(8,128)} %copy.204), calls=%async_computation.3 | async-start | bytes 4194304 | tf_op jit(solution)/shard_map/all_to_all | solution.py:108
  32.6 4.1 %copy.185 = f32[1,8,256,256]{3,1,0,2:T(8,128)} copy(f32[1,8,256,256]{3,2,1,0:T(8,128)} %get-tuple-element.78) | data formatting | bytes 4194304 | tf_op jit(solution)/shard_map/add | solution.py:91
  36.9 22.1 %all-to-all-done.3 = f32[1,8,256,256]{3,1,0,2:T(8,128)} async-done(((f32[1,8,256,256]{3,1,0,2:T(8,128)}), f32[1,8,256,256]{3,1,0,2:T(8,128)}, u32[]{:S(2)}, u32[]{:S(2)}) %all-to-all-start.3) | async-done | bytes 2097184 | tf_op jit(solution)/shard_map/all_to_all | solution.py:108
  58.9 5.2 %all-to-all-start = ((f32[1,8,256,256]{3,1,0,2:T(8,128)}), f32[1,8,256,256]{3,1,0,2:T(8,128)}, u32[]{:S(2)}, u32[]{:S(2)}) async-start(f32[1,8,256,256]{3,1,0,2:T(8,128)} %copy.185), calls=%async_computation | async-start | bytes 4194304 | tf_op jit(solution)/shard_map/all_to_all | solution.py:107
  65.0 2.2 copy.278
  69.8 20.7 %all-to-all-done = f32[1,8,256,256]{3,1,0,2:T(8,128)} async-done(((f32[1,8,256,256]{3,1,0,2:T(8,128)}), f32[1,8,256,256]{3,1,0,2:T(8,128)}, u32[]{:S(2)}, u32[]{:S(2)}) %all-to-all-start) | async-done | bytes 2097184 | tf_op jit(solution)/shard_map/all_to_all | solution.py:107
  90.5 2.3 copy.186
  95.2 7.9 %all-gather.2 = f32[4,1,8]{2,1,0:T(1,128)S(1)} all-gather(f32[1,1,8]{2,1,0:T(1,128)S(1)} %get-tuple-element.41), channel_id=1, replica_groups=mesh['grp_0'=4,'grp_1'=4,'mem'=8] {'grp_1'}, dimensions={0}, use_global_device_ids=true | all-gather | bytes 160 | tf_op jit(solution)/shard_map/all_gather | solution.py:26
  103.2 2.0 slice_add_fusion.11
  105.4 5.2 %all-gather = f32[4,1,8]{2,1,0:T(1,128)S(1)} all-gather(f32[1,1,8]{2,1,0:T(1,128)S(1)} %get-tuple-element.42), channel_id=1, replica_groups=mesh['grp_0'=4,'grp_1'=4,'mem'=8] {'grp_1'}, dimensions={0}, use_global_device_ids=true | all-gather | bytes 160 | tf_op jit(solution)/shard_map/all_gather | solution.py:26
  110.6 9.4 %all-gather.1 = f32[4,1,8]{2,1,0:T(1,128)S(1)} all-gather(f32[1,1,8]{2,1,0:T(1,128)S(1)} %get-tuple-element.66), channel_id=1, replica_groups=mesh['grp_0'=4,'grp_1'=4,'mem'=8] {'grp_0'}, dimensions={0}, use_global_device_ids=true | all-gather | bytes 160 | tf_op jit(solution)/shard_map/all_gather | solution.py:26
  120.0 5.4 %all-gather.3 = f32[4,1,8]{2,1,0:T(1,128)S(1)} all-gather(f32[1,1,8]{2,1,0:T(1,128)S(1)} %get-tuple-element.56), channel_id=1, replica_groups=mesh['grp_0'=4,'grp_1'=4,'mem'=8] {'grp_0'}, dimensions={0}, use_global_device_ids=true | all-gather | bytes 160 | tf_op jit(solution)/shard_map/all_gather | solution.py:26
  126.5 2.0 slice_add_fusion.19
  128.6 18.7 %all-gather.15.cloned.1.call-done = f32[4,8,32,256]{3,2,1,0:T(8,128)} async-done(((f32[1,8,32,256]{3,2,1,0:T(8,128)}), f32[4,8,32,256]{3,2,1,0:T(8,128)}) %all-gather.15.cloned.1.call-update) | async-done | bytes 1048592 | tf_op jit(solution)/shard_map/all_gather | solution.py:26
  147.3 2.8 %add_dynamic-update-slice_fusion.6 = (f32[8,8,32,256]{3,2,1,0:T(8,128)}, f32[1,8,32,256]{3,2,1,0:T(8,128)S(1)}) fusion(f32[8]{0:T(128)S(1)} %get-tuple-element.13, f32[1,8,32,256]{3,2,1,0:T(8,128)} %get-tuple-element.20, f32[8]{0:T(128)S(1)} %get-tuple-element.5, f32[8,1,8,32,256]{4,3,2,1,0:T(8,128)} %bitcast.342, pred[]{:T(512)S(6)} %lt.31, pred[]{:T(512)S(6)} %lt.30, ...), kind=kLoop, calls=%fused_computation.113 | loop fusion | flops 1835007 | bytes 3146088
  156.8 1.8 add_dynamic-update-slice_fusion
  159.3 7.0 %all-to-all-start.4 = ((f32[8,8,32,256]{3,2,1,0:T(8,128)}), f32[8,8,32,256]{3,2,1,0:T(8,128)}, u32[]{:S(2)}, u32[]{:S(2)}) async-start(f32[8,8,32,256]{3,2,1,0:T(8,128)} %constant_dynamic-update-slice_fusion.1), calls=%async_computation.4 | async-start | bytes 4194304 | tf_op jit(solution)/shard_map/all_to_all | solution.py:137
  166.3 7.9 %all-gather.11.cloned.1.call-done = f32[4,8,32,256]{3,2,1,0:T(8,128)} async-done(((f32[1,8,32,256]{3,2,1,0:T(8,128)}), f32[4,8,32,256]{3,2,1,0:T(8,128)}) %all-gather.11.cloned.1.call-update) | async-done | bytes 1048592 | tf_op jit(solution)/shard_map/all_gather | solution.py:26
  174.3 2.7 %constant_dynamic-update-slice_fusion = (f32[8,8,32,256]{3,2,1,0:T(8,128)}, f32[1,8,32,256]{3,2,1,0:T(8,128)S(1)}) fusion(pred[]{:T(512)S(6)} %gt.31, pred[]{:T(512)S(6)} %gt.30, pred[]{:T(512)S(6)} %gt.29, f32[8]{0:T(128)S(1)} %copy-done.30, f32[4,8,32,256]{3,2,1,0:T(8,128)} %all-gather.11.cloned.1.call-done, f32[8]{0:T(128)S(1)} %copy-done.28, ...), kind=kLoop, calls=%fused_computation.122 | loop fusion | flops 1572863 | bytes 2621736
  182.7 10.0 %all-to-all-done.4 = f32[8,8,32,256]{3,2,1,0:T(8,128)} async-done(((f32[8,8,32,256]{3,2,1,0:T(8,128)}), f32[8,8,32,256]{3,2,1,0:T(8,128)}, u32[]{:S(2)}, u32[]{:S(2)}) %all-to-all-start.4) | async-done | bytes 2097184 | tf_op jit(solution)/shard_map/all_to_all | solution.py:137
  192.6 5.2 %all-to-all-start.2 = ((f32[8,8,32,256]{3,2,1,0:T(8,128)}), f32[8,8,32,256]{3,2,1,0:T(8,128)}, u32[]{:S(2)}, u32[]{:S(2)}) async-start(f32[8,8,32,256]{3,2,1,0:T(8,128)} %add_dynamic-update-slice_fusion.7), calls=%async_computation.2 | async-start | bytes 4194304 | tf_op jit(solution)/shard_map/all_to_all | solution.py:136
  197.9 3.0 %fusion.12 = bf16[2,8,128,128]{3,2,1,0:T(8,128)(2,1)} fusion(bf16[2,128,8,256]{3,2,1,0:T(8,128)(2,1)} %bitcast.354, bf16[2,128,8,256]{3,2,1,0:T(8,128)(2,1)} %bitcast.350, f32[2,8,128]{2,1,0:T(8,128)S(1)} %reduce_window_sum.11, pred[128,128]{1,0:T(8,128)(4,1)S(1)} %iota_compare_fusion), kind=kOutput, calls=%fused_computation.26 | convolution fusion | flops 135528448 | bytes 2646016 | tf_op jit(solution)/shard_map/bthe,bshe->bhts/dot_general | solution.py:56
  200.8 1.8 copy.207
  202.7 2.4 fusion.22
  205.1 2.1 fusion.26
  207.2 17.0 %all-to-all-done.2 = f32[8,8,32,256]{3,2,1,0:T(8,128)} async-done(((f32[8,8,32,256]{3,2,1,0:T(8,128)}), f32[8,8,32,256]{3,2,1,0:T(8,128)}, u32[]{:S(2)}, u32[]{:S(2)}) %all-to-all-start.2) | async-done | bytes 2097184 | tf_op jit(solution)/shard_map/all_to_all | solution.py:136
  224.2 1.9 copy.195
  232.4 3.2 %fusion.3 = bf16[2,128,8,256]{3,1,2,0:T(8,128)(2,1)} fusion(f32[2,8,256,128]{2,3,1,0:T(8,128)} %fusion.26, f32[2,128,8]{1,2,0:T(8,128)S(1)} %get-tuple-element.40, bf16[2,128,8,256]{3,2,1,0:T(8,128)(2,1)S(1)} %bitcast.348, bf16[2,128,8,256]{3,2,1,0:T(8,128)(2,1)S(1)} %bitcast.335, bf16[2,128,8,256]{3,2,1,0:T(8,128)(2,1)S(1)} %bitcast.352, ...), kind=kOutput, calls=%fused_computation.10 | convolution fusion | flops 271843328 | bytes 6324224 | tf_op jit(solution)/shard_map/bhts,bthe->bshe/dot_general | solution.py:70
  235.6 1.8 copy.218
  (122 shorter events, 37.3 us)
Async XLA Ops:
  7.2 10.1 %copy-start.17 = (bf16[256,2048]{1,0:T(8,128)(2,1)S(1)}, bf16[256,2048]{1,0:T(8,128)(2,1)}, u32[]{:S(2)}) copy-start(bf16[256,2048]{1,0:T(8,128)(2,1)} %param.8) | copy-start | bytes 3145732
  9.3 18.5 %all-to-all-start.1 = ((f32[1,8,8,1]{1,3,0,2:T(1,128)}), f32[1,8,8,1]{1,3,0,2:T(1,128)S(1)}, u32[]{:S(2)}, u32[]{:S(2)}) async-start(f32[1,8,8,1]{1,3,0,2:T(1,128)} %broadcast_in_dim.20), calls=%async_computation.1 | async-start | bytes 8192 | tf_op jit(solution)/shard_map/all_to_all | solution.py:106
  17.3 2.3 copy-start.3
  17.6 2.0 copy-start.5
  18.0 3.0 %copy-start.7 = (bf16[32,8,8,256]{3,2,1,0:T(8,128)(2,1)}, bf16[32,8,8,256]{3,2,1,0:T(8,128)(2,1)S(1)}, u32[]{:S(2)}) copy-start(bf16[32,8,8,256]{3,2,1,0:T(8,128)(2,1)S(1)} %copy.237) | copy-start | bytes 3145732
  27.8 31.1 %all-to-all-start.3 = ((f32[1,8,256,256]{3,1,0,2:T(8,128)}), f32[1,8,256,256]{3,1,0,2:T(8,128)}, u32[]{:S(2)}, u32[]{:S(2)}) async-start(f32[1,8,256,256]{3,1,0,2:T(8,128)} %copy.204), calls=%async_computation.3 | async-start | bytes 4194304 | tf_op jit(solution)/shard_map/all_to_all | solution.py:108
  58.9 31.5 %all-to-all-start = ((f32[1,8,256,256]{3,1,0,2:T(8,128)}), f32[1,8,256,256]{3,1,0,2:T(8,128)}, u32[]{:S(2)}, u32[]{:S(2)}) async-start(f32[1,8,256,256]{3,1,0,2:T(8,128)} %copy.185), calls=%async_computation | async-start | bytes 4194304 | tf_op jit(solution)/shard_map/all_to_all | solution.py:107
  64.1 39.1 %all-gather.13.cloned.1.call-start = ((), (), s32[]{:S(2)}) async-start(), calls=%async_computation.7 | async-start | bytes 1310720 | tf_op jit(solution)/shard_map/all_gather | solution.py:26
  69.8 56.7 %all-gather.9.cloned.1.call-start = ((), (), s32[]{:S(2)}) async-start(), calls=%async_computation.5 | async-start | bytes 1310720 | tf_op jit(solution)/shard_map/all_gather | solution.py:26
  95.2 52.1 %all-gather.15.cloned.1.call-start = ((), (), s32[]{:S(2)}) async-start(), calls=%async_computation.8 | async-start | bytes 1310720 | tf_op jit(solution)/shard_map/all_gather | solution.py:26
  105.3 68.9 %all-gather.11.cloned.1.call-start = ((), (), s32[]{:S(2)}) async-start(), calls=%async_computation.6 | async-start | bytes 1310720 | tf_op jit(solution)/shard_map/all_gather | solution.py:26
  147.3 2.8 %copy-start.15 = (f32[1,8,32,256]{3,2,1,0:T(8,128)S(1)}, f32[1,8,32,256]{3,2,1,0:T(8,128)}, u32[]{:S(2)}) copy-start(f32[1,8,32,256]{3,2,1,0:T(8,128)} %get-tuple-element.20) | copy-start | bytes 786436
  147.3 4.3 %copy-start.14 = (f32[1,8,32,256]{3,2,1,0:T(8,128)S(1)}, f32[1,8,32,256]{3,2,1,0:T(8,128)}, u32[]{:S(2)}) copy-start(f32[1,8,32,256]{3,2,1,0:T(8,128)} %get-tuple-element.21) | copy-start | bytes 786436
  147.3 6.0 %copy-start.25 = (f32[8]{0:T(128)S(1)}, f32[8]{0:T(128)}, u32[]{:S(2)}) copy-start(f32[8]{0:T(128)} %get-tuple-element.16) | copy-start | bytes 100
  150.1 4.1 %copy-start.13 = (f32[1,8,32,256]{3,2,1,0:T(8,128)S(1)}, f32[1,8,32,256]{3,2,1,0:T(8,128)}, u32[]{:S(2)}) copy-start(f32[1,8,32,256]{3,2,1,0:T(8,128)} %get-tuple-element.22) | copy-start | bytes 786436
  150.1 5.8 %copy-start.24 = (f32[8]{0:T(128)S(1)}, f32[8]{0:T(128)}, u32[]{:S(2)}) copy-start(f32[8]{0:T(128)} %get-tuple-element.18) | copy-start | bytes 100
  159.3 15.0 %copy-start.26 = (f32[8]{0:T(128)S(1)}, f32[8]{0:T(128)}, u32[]{:S(2)}) copy-start(f32[8]{0:T(128)} %get-tuple-element.59) | copy-start | bytes 100
  159.3 15.0 %copy-start.27 = (f32[8]{0:T(128)S(1)}, f32[8]{0:T(128)}, u32[]{:S(2)}) copy-start(f32[8]{0:T(128)} %get-tuple-element.61) | copy-start | bytes 100
  159.3 15.0 %copy-start.28 = (f32[8]{0:T(128)S(1)}, f32[8]{0:T(128)}, u32[]{:S(2)}) copy-start(f32[8]{0:T(128)} %get-tuple-element.62) | copy-start | bytes 100
  159.3 15.0 %copy-start.29 = (f32[8]{0:T(128)S(1)}, f32[8]{0:T(128)}, u32[]{:S(2)}) copy-start(f32[8]{0:T(128)} %get-tuple-element.63) | copy-start | bytes 100
  159.3 15.0 %copy-start.30 = (f32[8]{0:T(128)S(1)}, f32[8]{0:T(128)}, u32[]{:S(2)}) copy-start(f32[8]{0:T(128)} %get-tuple-element.64) | copy-start | bytes 100
  159.3 33.3 %all-to-all-start.4 = ((f32[8,8,32,256]{3,2,1,0:T(8,128)}), f32[8,8,32,256]{3,2,1,0:T(8,128)}, u32[]{:S(2)}, u32[]{:S(2)}) async-start(f32[8,8,32,256]{3,2,1,0:T(8,128)} %constant_dynamic-update-slice_fusion.1), calls=%async_computation.4 | async-start | bytes 4194304 | tf_op jit(solution)/shard_map/all_to_all | solution.py:137
  166.3 11.5 %copy-start.23 = (f32[8]{0:T(128)S(1)}, f32[8]{0:T(128)}, u32[]{:S(2)}) copy-start(f32[8]{0:T(128)} %get-tuple-element.48) | copy-start | bytes 100
  174.2 2.8 %copy-start.1 = (f32[1,8,256,256]{3,2,1,0:T(8,128)S(1)}, f32[1,8,256,256]{3,2,1,0:T(8,128)}, u32[]{:S(2)}) copy-start(f32[1,8,256,256]{3,2,1,0:T(8,128)} %copy-done) | copy-start | bytes 6291460
  174.2 3.6 %copy-start.12 = (f32[1,8,32,256]{3,2,1,0:T(8,128)S(1)}, f32[1,8,32,256]{3,2,1,0:T(8,128)}, u32[]{:S(2)}) copy-start(f32[1,8,32,256]{3,2,1,0:T(8,128)} %get-tuple-element.36) | copy-start | bytes 786436
  174.3 5.2 %copy-start.11 = (f32[1,8,32,256]{3,2,1,0:T(8,128)S(1)}, f32[1,8,32,256]{3,2,1,0:T(8,128)}, u32[]{:S(2)}) copy-start(f32[1,8,32,256]{3,2,1,0:T(8,128)} %get-tuple-element.35) | copy-start | bytes 786436
  174.3 5.2 %copy-start.22 = (f32[8]{0:T(128)S(1)}, f32[8]{0:T(128)}, u32[]{:S(2)}) copy-start(f32[8]{0:T(128)} %get-tuple-element.46) | copy-start | bytes 100
  177.0 4.0 %copy-start.21 = (f32[8]{0:T(128)S(1)}, f32[8]{0:T(128)}, u32[]{:S(2)}) copy-start(f32[8]{0:T(128)} %get-tuple-element.44) | copy-start | bytes 100
  182.7 15.2 %copy-start.20 = (f32[1,8]{1,0:T(1,128)S(1)}, f32[1,8]{1,0:T(1,128)}, u32[]{:S(2)}) copy-start(f32[1,8]{1,0:T(1,128)} %get-tuple-element.72) | copy-start | bytes 100
  192.6 31.5 %all-to-all-start.2 = ((f32[8,8,32,256]{3,2,1,0:T(8,128)}), f32[8,8,32,256]{3,2,1,0:T(8,128)}, u32[]{:S(2)}, u32[]{:S(2)}) async-start(f32[8,8,32,256]{3,2,1,0:T(8,128)} %add_dynamic-update-slice_fusion.7), calls=%async_computation.2 | async-start | bytes 4194304 | tf_op jit(solution)/shard_map/all_to_all | solution.py:136
  207.2 18.9 %copy-start.6 = (bf16[32,8,8,256]{3,2,1,0:T(8,128)(2,1)S(1)}, bf16[32,8,8,256]{3,2,1,0:T(8,128)(2,1)}, u32[]{:S(2)}) copy-start(bf16[32,8,8,256]{3,2,1,0:T(8,128)(2,1)} %copy-done.5) | copy-start | bytes 3145732
  224.2 2.2 copy-start.9
  (8 other events, 13.4 us)
Sparse Core Ops, SparseCore 0:
  69.9 24.2 all-gather.12
  96.4 24.4 all-gather.8
  122.6 24.6 all-gather.14
  149.4 24.7 all-gather.10
where the time goes:
time: 246 us; the launch traced here: 245 us
  waiting for transfers between devices  96.4 us (39%)
  other arithmetic  31.9 us (13%)
  local copies, waits for them, and re-layouts  31.4 us (13%)
  starting transfers between devices  28.1 us (11%)
  blocking collectives  27.9 us (11%)
  matrix products  15.4 us (6%)
  between operations  14.1 us (6%)
    all_gather x4, blocking collectives, entering(): pieces = jax.tree.map(lambda part: lax.all_gather(part, axis), total)  27.9 us
    all_gather x4, waiting for transfers between devices, entering(): pieces = jax.tree.map(lambda part: lax.all_gather(part, axis), total)  26.7 us
    all_to_all x1, waiting for transfers between devices, body(): lax.all_to_all(running[None], 'mem', split_axis=2, concat_axis=0, tiled=T...  22.1 us
    all_to_all x1, waiting for transfers between devices, body(): lax.all_to_all(forward_total[None], 'mem', split_axis=2, concat_axis=0, t...  20.7 us
    unnamed x15, other arithmetic  18.8 us
    all_to_all x1, waiting for transfers between devices, body(): lax.all_to_all(first_stack, 'mem', split_axis=0, concat_axis=2, tiled=True)  17 us
    unnamed x69, local copies, waits for them, and re-layouts  11.1 us
    all_to_all x1, waiting for transfers between devices, body(): lax.all_to_all(second_stack, 'mem', split_axis=0, concat_axis=2, tiled=True)  9.97 us
  transfers between devices with their start and end apart: 9, of which 6 were waited for; matrix products, arithmetic and copies ran while one was open for 24% of the time, Pallas kernels for 0%

commit v1 on v0

v1 whole, which is shorter than its diff:
```python
import functools

import jax
import jax.numpy as jnp
from jax import lax
from jax.experimental import pallas as pl
from jax.experimental.pallas import tpu as pltpu
from jax.sharding import Mesh
from jax.sharding import PartitionSpec as P

H = 8
DK = 256
DV = 256
BLOCK = 128
AXES = ("z", "y", "x", "c")
MESH = pl.DeviceIdType.MESH
F32 = jnp.float32
BF16 = jnp.bfloat16
SHARE = 32


def two(a):
    return jnp.concatenate([a, a], axis=1)


def dot(a, b, ca, cb):
    return lax.dot_general(a, b, (((ca,), (cb,)), ((), ())), preferred_element_type=F32)


def kernel(q, k, v, g, ld, dq, dk, dv, col, en, inner, u0s, v1s, tc, pt, ct, xu, yb, pln, zb,
           sd, xd, sp, fs, dc, dx, dy, dz, wc, wx, wy, wz, s_small, r_small, s_t, r_t, s_xu, r_xu,
           s_y, r_y, s_z, r_z, s_xd, r_xd, s_f, r_f):
    iz, iy, ix, ic = (lax.axis_index(a) for a in AXES)
    other = 1 - ic

    def peer(axis, i):
        if axis == "c":
            return {"c": other}
        return {axis: lax.rem(lax.axis_index(axis) + i, 4)}

    barrier = pltpu.get_barrier_semaphore()
    pl.semaphore_signal(barrier, inc=1, device_id=peer("c", 1), device_id_type=MESH)
    for axis in ("x", "y", "z"):
        for i in (1, 2, 3):
            pl.semaphore_signal(barrier, inc=1, device_id=peer(axis, i), device_id_type=MESH)

    def remote(src, dst, ssem, rsem, axis, i):
        return pltpu.make_async_remote_copy(
            src_ref=src, dst_ref=dst, send_sem=ssem, recv_sem=rsem,
            device_id=peer(axis, i), device_id_type=MESH)

    def c_small():
        return remote(dc.at[ic], dc.at[ic], s_small.at[0], r_small.at[0], "c", 1)

    def small(buf, mine, base, axis, i):
        return remote(buf.at[mine], buf.at[mine], s_small.at[base + i], r_small.at[base + i], axis, i)

    def t_copy(h):
        rows = pl.ds(pl.multiple_of(128 * other, 128), 128)
        return remote(tc.at[h, :, rows], pt.at[h], s_t.at[h], r_t.at[h], "c", 1)

    def xu_copy(h, i):
        return remote(ct.at[h, lax.rem(ix + i, 4)], xu.at[h, ix], s_xu.at[h, i - 1], r_xu.at[h, i - 1], "x", i)

    def y_copy(h, i):
        return remote(yb.at[h, iy], yb.at[h, iy], s_y.at[h, i - 1], r_y.at[h, i - 1], "y", i)

    def z_copy(h, i):
        part = lax.div(iz + i, 4)
        return remote(pln.at[h, part], zb.at[h, iz], s_z.at[h, i - 1], r_z.at[h, i - 1], "z", i)

    def xd_copy(h, i):
        return remote(sd.at[h, lax.rem(ix + i, 4)], xd.at[h, ix], s_xd.at[h, i - 1], r_xd.at[h, i - 1], "x", i)

    def f_copy(h):
        rows = pl.ds(pl.multiple_of(128 * ic, 128), 128)
        return remote(sp.at[h], fs.at[h, :, rows], s_f.at[h], r_f.at[h], "c", 1)

    ii = lax.broadcasted_iota(jnp.int32, (BLOCK, BLOCK), 0)
    jj = lax.broadcasted_iota(jnp.int32, (BLOCK, BLOCK), 1)
    upper = jnp.where(ii <= jj, 1.0, 0.0).astype(F32)
    for b in range(2):
        cum = lax.dot_general(ld[:, b * BLOCK:(b + 1) * BLOCK], upper, (((1,), (0,)), ((), ())),
                              precision=lax.Precision.HIGHEST, preferred_element_type=F32)
        for h in range(H):
            col[h, b] = jnp.broadcast_to(cum[h:h + 1, :], (BLOCK, BLOCK)).T
        en[b] = jnp.broadcast_to(cum[:, BLOCK - 1:BLOCK], (H, DV))
    dc[ic] = en[0] + en[1]

    pl.semaphore_wait(barrier, 10)
    c_small().start()

    def products(h):
        cols = pl.ds(pl.multiple_of(h * DK, DK), DK)
        parts = []
        for b in range(2):
            rows = slice(b * BLOCK, (b + 1) * BLOCK)
            cb = col[h, b]
            hf = two(jnp.exp(cb))
            tf = two(jnp.exp(cb[BLOCK - 1:BLOCK, :] - cb))
            kd = (k[rows, cols].astype(F32) * tf).astype(BF16)
            qd = (q[rows, cols].astype(F32) * hf).astype(BF16)
            parts.append((dot(kd, v[rows, cols], 0, 0), dot(qd, g[rows, cols], 0, 0)))
        e0 = jnp.exp(en[0, pl.ds(h, 1), :])
        e1 = jnp.exp(en[1, pl.ds(h, 1), :])
        u0s[h] = parts[0][0]
        v1s[h] = parts[1][1]
        tc[h, 0] = e1 * parts[0][0] + parts[1][0]
        tc[h, 1] = e0 * parts[1][1] + parts[0][1]
        t_copy(h).start()

    def chip_total(h):
        t_copy(h).wait_recv()
        for s in range(4):
            for d in range(2):
                mine = pl.ds(pl.multiple_of(128 * ic + SHARE * s, SHARE), SHARE)
                ct[h, s, d] = (wc[2 * d, pl.ds(h, 1), :] * tc[h, d, mine, :]
                               + wc[2 * d + 1, pl.ds(h, 1), :] * pt[h, d, pl.ds(SHARE * s, SHARE), :])
        xu[h, ix] = ct[h, ix]
        for i in (1, 2, 3):
            xu_copy(h, i).start()

    def chain_total(buf, w, h):
        f = buf[h, 0, 0]
        for j in (1, 2, 3):
            f = w[j, pl.ds(h, 1), :] * f + buf[h, j, 0]
        r = buf[h, 3, 1]
        for j in (2, 1, 0):
            r = w[j, pl.ds(h, 1), :] * r + buf[h, j, 1]
        return f, r

    def row_total(h):
        for i in (1, 2, 3):
            xu_copy(h, i).wait_recv()
        f, r = chain_total(xu, wx, h)
        yb[h, iy, 0] = f
        yb[h, iy, 1] = r
        for i in (1, 2, 3):
            y_copy(h, i).start()

    def plane_total(h):
        for i in (1, 2, 3):
            y_copy(h, i).wait_recv()
        f, r = chain_total(yb, wy, h)
        pln[h, 0] = f
        pln[h, 1] = r
        zb[h, iz] = jnp.zeros((SHARE, DV), F32)
        for i in (1, 2, 3):
            z_copy(h, i).start()

    def incoming(h):
        for i in (1, 2, 3):
            z_copy(h, i).wait_recv()
        f = jnp.zeros((SHARE, DV), F32)
        r = jnp.zeros((SHARE, DV), F32)
        for j in range(4):
            zj = zb[h, j]
            f = f + wz[j, pl.ds(h, 1), :] * zj
            r = r + wz[4 + j, pl.ds(h, 1), :] * zj
        for j in range(4):
            f = f + wz[8 + j, pl.ds(h, 1), :] * yb[h, j, 0]
            r = r + wz[12 + j, pl.ds(h, 1), :] * yb[h, j, 1]
        for j in range(4):
            sd[h, j, 0] = f
            if j < 3:
                f = wx[j, pl.ds(h, 1), :] * f + xu[h, j, 0]
        for j in (3, 2, 1, 0):
            sd[h, j, 1] = r
            if j > 0:
                r = wx[j, pl.ds(h, 1), :] * r + xu[h, j, 1]
        xd[h, ix] = sd[h, ix]
        for i in (1, 2, 3):
            xd_copy(h, i).start()

    def core_state(h):
        for i in (1, 2, 3):
            xd_copy(h, i).wait_recv()
        for s in range(4):
            for d in range(2):
                mine = pl.ds(pl.multiple_of(128 * ic + SHARE * s, SHARE), SHARE)
                st = xd[h, s, d]
                fs[h, d, mine, :] = (wc[4 + 2 * d, pl.ds(h, 1), :] * st
                                     + wc[5 + 2 * d, pl.ds(h, 1), :] * pt[h, d, pl.ds(SHARE * s, SHARE), :])
                sp[h, d, pl.ds(SHARE * s, SHARE), :] = (wc[8 + 2 * d, pl.ds(h, 1), :] * st
                                                        + wc[9 + 2 * d, pl.ds(h, 1), :] * tc[h, d, mine, :])
        f_copy(h).start()

    def inside(h):
        cols = pl.ds(pl.multiple_of(h * DK, DK), DK)
        for b in range(2):
            rows = slice(b * BLOCK, (b + 1) * BLOCK)
            cb = col[h, b]
            spread = cb - cb.T
            decay = jnp.where(jj <= ii, jnp.exp(jnp.where(jj <= ii, spread, 0.0)), 0.0)
            qb, kb, vb, gb = q[rows, cols], k[rows, cols], v[rows, cols], g[rows, cols]
            wg = (dot(gb, vb, 1, 1) * decay).astype(BF16)
            wv = (dot(qb, kb, 1, 1) * decay).astype(BF16)
            inner[h, 0, rows, :] = dot(wg, kb, 1, 0)
            inner[h, 1, rows, :] = dot(wg, qb, 0, 0)
            inner[h, 2, rows, :] = dot(wv, gb, 0, 0)

    def outputs(h):
        f_copy(h).wait_recv()
        cols = pl.ds(pl.multiple_of(h * DK, DK), DK)
        e0 = jnp.exp(en[0, pl.ds(h, 1), :])
        e1 = jnp.exp(en[1, pl.ds(h, 1), :])
        sf = fs[h, 0]
        sr = fs[h, 1]
        states = (sf.astype(BF16), (e0 * sf + u0s[h]).astype(BF16))
        grads = ((e1 * sr + v1s[h]).astype(BF16), sr.astype(BF16))
        scale = DK ** -0.5
        for b in range(2):
            rows = slice(b * BLOCK, (b + 1) * BLOCK)
            cb = col[h, b]
            hf = two(jnp.exp(cb))
            tf = two(jnp.exp(cb[BLOCK - 1:BLOCK, :] - cb))
            oq = dot(g[rows, cols], states[b], 1, 1)
            ok = dot(v[rows, cols], grads[b], 1, 1)
            ov = dot(k[rows, cols], grads[b], 1, 0)
            dq[rows, cols] = (scale * (inner[h, 0, rows, :] + hf * oq)).astype(BF16)
            dk[rows, cols] = (scale * (inner[h, 1, rows, :] + tf * ok)).astype(BF16)
            dv[rows, cols] = (scale * (inner[h, 2, rows, :] + tf * ov)).astype(BF16)

    def core_weights():
        c_small().wait_recv()
        me = dc[ic]
        ot = dc[other]
        first = ic == 0
        one = jnp.ones((H, DV), F32)
        zero = jnp.zeros((H, DV), F32)
        eme = jnp.exp(me)
        eot = jnp.exp(ot)
        wc[0] = jnp.where(first, eot, one)
        wc[1] = jnp.where(first, one, eme)
        wc[2] = jnp.where(first, one, eot)
        wc[3] = jnp.where(first, eme, one)
        wc[4] = jnp.where(first, one, eot)
        wc[5] = jnp.where(first, zero, one)
        wc[6] = jnp.where(first, eot, one)
        wc[7] = jnp.where(first, one, zero)
        wc[8] = jnp.where(first, eme, one)
        wc[9] = jnp.where(first, one, zero)
        wc[10] = jnp.where(first, one, eme)
        wc[11] = jnp.where(first, zero, one)
        dx[ix] = me + ot
        for i in (1, 2, 3):
            small(dx, ix, 0, "x", i).start()

    def row_weights():
        for i in (1, 2, 3):
            small(dx, ix, 0, "x", i).wait_recv()
        for j in range(4):
            wx[j] = jnp.exp(dx[j])
        dy[iy] = (dx[0] + dx[1]) + (dx[2] + dx[3])
        for i in (1, 2, 3):
            small(dy, iy, 3, "y", i).start()

    def plane_weights():
        for i in (1, 2, 3):
            small(dy, iy, 3, "y", i).wait_recv()
        for j in range(4):
            wy[j] = jnp.exp(dy[j])
        dz[iz] = (dy[0] + dy[1]) + (dy[2] + dy[3])
        for i in (1, 2, 3):
            small(dz, iz, 6, "z", i).start()

    def prefix_weights():
        for i in (1, 2, 3):
            small(dz, iz, 6, "z", i).wait_recv()
        zero = jnp.zeros((H, DV), F32)
        before = zero
        after = zero
        for j in range(4):
            before = before + jnp.where(j < iy, dy[j], 0.0)
            after = after + jnp.where(j > iy, dy[j], 0.0)
        for j in range(4):
            zf, zr, yf, yr = before, after, zero, zero
            for m in range(4):
                if m > j:
                    zf = zf + jnp.where(m < iz, dz[m], 0.0)
                    yf = yf + jnp.where(m < iy, dy[m], 0.0)
                if m < j:
                    zr = zr + jnp.where(m > iz, dz[m], 0.0)
                    yr = yr + jnp.where(m > iy, dy[m], 0.0)
            wz[j] = jnp.where(j < iz, jnp.exp(zf), 0.0)
            wz[4 + j] = jnp.where(j > iz, jnp.exp(zr), 0.0)
            wz[8 + j] = jnp.where(j < iy, jnp.exp(yf), 0.0)
            wz[12 + j] = jnp.where(j > iy, jnp.exp(yr), 0.0)

    def first_loop(t, carry):
        @pl.when(t < H)
        def _():
            products(t)

        @pl.when(t == 0)
        def _():
            core_weights()

        @pl.when(t == 3)
        def _():
            row_weights()

        @pl.when(t == 6)
        def _():
            plane_weights()

        @pl.when(t >= 1)
        def _():
            chip_total(t - 1)
        return carry

    lax.fori_loop(0, H + 1, first_loop, 0)
    prefix_weights()

    def second_loop(t, carry):
        @pl.when(t < H)
        def _():
            row_total(t)

        @pl.when((t >= 1) & (t < H + 1))
        def _():
            plane_total(t - 1)

        @pl.when(t >= 2)
        def _():
            incoming(t - 2)

        @pl.when(t < H)
        def _():
            inside(t)
        return carry

    lax.fori_loop(0, H + 2, second_loop, 0)

    def third_loop(t, carry):
        @pl.when(t < H)
        def _():
            core_state(t)

        @pl.when(t >= 1)
        def _():
            outputs(t - 1)
        return carry

    lax.fori_loop(0, H + 1, third_loop, 0)

    def drain(h, carry):
        t_copy(h).wait_send()
        f_copy(h).wait_send()
        for i in (1, 2, 3):
            xu_copy(h, i).wait_send()
            y_copy(h, i).wait_send()
            z_copy(h, i).wait_send()
            xd_copy(h, i).wait_send()
        return carry

    lax.fori_loop(0, H, drain, 0)
    c_small().wait_send()
    for i in (1, 2, 3):
        small(dx, ix, 0, "x", i).wait_send()
        small(dy, iy, 3, "y", i).wait_send()
        small(dz, iz, 6, "z", i).wait_send()


def body(queries, keys, values, grad_out, log_decay):
    vmem = pl.BlockSpec(memory_space=pltpu.VMEM)
    shape = jax.ShapeDtypeStruct(queries.shape, BF16)
    tile = pltpu.VMEM
    dma = pltpu.SemaphoreType.DMA
    return pl.pallas_call(
        kernel,
        out_shape=(shape, shape, shape),
        in_specs=[vmem] * 5,
        out_specs=(vmem, vmem, vmem),
        scratch_shapes=[
            tile((H, 2, BLOCK, BLOCK), F32),
            tile((2, H, DV), F32),
            tile((H, 3, 2 * BLOCK, DK), F32),
            tile((H, DK, DV), F32),
            tile((H, DK, DV), F32),
            tile((H, 2, DK, DV), F32),
            tile((H, 2, DK // 2, DV), F32),
            tile((H, 4, 2, SHARE, DV), F32),
            tile((H, 4, 2, SHARE, DV), F32),
            tile((H, 4, 2, SHARE, DV), F32),
            tile((H, 2, SHARE, DV), F32),
            tile((H, 4, SHARE, DV), F32),
            tile((H, 4, 2, SHARE, DV), F32),
            tile((H, 4, 2, SHARE, DV), F32),
            tile((H, 2, DK // 2, DV), F32),
            tile((H, 2, DK, DV), F32),
            tile((2, H, DV), F32),
            tile((4, H, DV), F32),
            tile((4, H, DV), F32),
            tile((4, H, DV), F32),
            tile((12, H, DV), F32),
            tile((4, H, DV), F32),
            tile((4, H, DV), F32),
            tile((16, H, DV), F32),
            dma((10,)), dma((10,)),
            dma((H,)), dma((H,)),
            dma((H, 3)), dma((H, 3)),
            dma((H, 3)), dma((H, 3)),
            dma((H, 3)), dma((H, 3)),
            dma((H, 3)), dma((H, 3)),
            dma((H,)), dma((H,)),
        ],
        compiler_params=pltpu.CompilerParams(
            collective_id=0, has_side_effects=True, vmem_limit_bytes=60 * 1024 * 1024),
    )(queries, keys, values, grad_out, log_decay)


def solution(mesh):
    torus = Mesh(mesh.devices.reshape(4, 4, 4, 2), AXES)
    rows = P(AXES, None)
    return jax.shard_map(
        body,
        mesh=torus,
        in_specs=(rows, rows, rows, rows, P(None, AXES)),
        out_specs=(rows, rows, rows),
        check_vma=False,
    )
```

time: 246 us -> 70.4 us (0.29)
  waiting for transfers between devices: 96.4 us -> 0 us
  Pallas kernels: 0 us -> 64.6 us
  other arithmetic: 31.9 us -> 0 us
  starting transfers between devices: 28.1 us -> 0 us
  blocking collectives: 27.9 us -> 0 us
  local copies, waits for them, and re-layouts: 31.4 us -> 4.97 us
  matrix products: 15.4 us -> 0 us
  between operations: 14.1 us -> 0.65 us
    all_to_all x5 -> x0, waiting for transfers between devices: 69.7 us -> none  [the longest x1 22.1 us: body(): lax.all_to_all(running[None], 'mem', split_axis=2, concat_axis=0, tiled=T...]
    pallas_call x0 -> x1, Pallas kernels: none -> 64.6 us  [body(): pl.pallas_call(kernel, out_shape=(shape, shape, shape), in_specs=[vmem] *...]
    all_to_all x5 -> x0, starting transfers between devices: 28 us -> none  [the longest x1 7.01 us: body(): lax.all_to_all(second_stack, 'mem', split_axis=0, concat_axis=2, tiled=True)]
    all_gather x4 -> x0, blocking collectives: 27.9 us -> none  [entering(): pieces = jax.tree.map(lambda part: lax.all_gather(part, axis), total)]
    all_gather x4 -> x0, waiting for transfers between devices: 26.7 us -> none  [entering(): pieces = jax.tree.map(lambda part: lax.all_gather(part, axis), total)]
    unnamed x15 -> x0, other arithmetic: 18.8 us -> none
    dot_general x9 -> x0, matrix products: 15.4 us -> none  [the longest x1 3.18 us: body(): jnp.einsum('bhts,bthe->bshe', weight_value, grad_blocks, preferred_elemen...]
    add x5 -> x0, other arithmetic: 9.06 us -> none  [the longest x4 6.2 us: chain(): late_state + late_decay[:, None, None] * early_state]
  transfers between devices with their start and end apart: 9 -> 0, of which waited for: 6 -> 0; matrix products, arithmetic and copies ran while one was open for 24% -> 0% of each run, Pallas kernels for 0% -> 0%
where the time goes in v1:
time: 70.4 us; the launch traced here: 70.2 us
  Pallas kernels  64.6 us (92%)
  local copies, waits for them, and re-layouts  4.97 us (7%)
    pallas_call x1, Pallas kernels, body(): pl.pallas_call(kernel, out_shape=(shape, shape, shape), in_specs=[vmem] *...  64.6 us
    unnamed x7, local copies, waits for them, and re-layouts  4.97 us

profile of v1, /device:TPU:1, one launch (start us, length us, event | category | flops | bytes accessed | tf_op | source)
XLA Modules:
  0.0 70.2 jit_solution(1302547051071604268)
XLA Ops:
  0.6 64.6 %shard_map.76 = (bf16[256,2048]{1,0:T(8,128)(2,1)}, bf16[256,2048]{1,0:T(8,128)(2,1)}, bf16[256,2048]{1,0:T(8,128)(2,1)}) custom-call(bf16[256,2048]{1,0:T(8,128)(2,1)} %q.1, bf16[256,2048]{1,0:T(8,128)(2,1)} %k.1, bf16[256,2048]{1,0:T(8,128)(2,1)} %v.1, bf16[256,2048]{1,0:T(8,128)(2,1)} %g.1, f32[8,256]{1,0:T(8,128)} %ld.1), custom_call_target="tpu_custom_call" | custom-call | tf_op jit(solution)/shard_map/pallas_call | solution.py:370
  65.3 0.0 copy-start.1
  65.3 2.4 %copy.11 = bf16[256,2048]{1,0:T(8,128)(2,1)} copy(bf16[256,2048]{1,0:T(8,128)(2,1)} %get-tuple-element.6) | data formatting | bytes 2097152
  67.7 0.0 copy-done.1
  67.7 0.0 copy-start
  67.7 1.0 %copy.12 = bf16[256,2048]{1,0:T(8,128)(2,1)} copy(bf16[256,2048]{1,0:T(8,128)(2,1)S(1)} %copy-done.1) | data formatting | bytes 2097152
  68.6 0.6 copy-done
  69.3 1.0 %copy.13 = bf16[256,2048]{1,0:T(8,128)(2,1)} copy(bf16[256,2048]{1,0:T(8,128)(2,1)S(1)} %copy-done) | data formatting | bytes 2097152
Async XLA Ops:
  65.3 2.4 %copy-start.1 = (bf16[256,2048]{1,0:T(8,128)(2,1)S(1)}, bf16[256,2048]{1,0:T(8,128)(2,1)}, u32[]{:S(2)}) copy-start(bf16[256,2048]{1,0:T(8,128)(2,1)} %get-tuple-element.7) | copy-start | bytes 3145732
  67.7 1.6 %copy-start = (bf16[256,2048]{1,0:T(8,128)(2,1)S(1)}, bf16[256,2048]{1,0:T(8,128)(2,1)}, u32[]{:S(2)}) copy-start(bf16[256,2048]{1,0:T(8,128)(2,1)} %get-tuple-element.8) | copy-start | bytes 3145732

commit v2 on v1

--- a/solution.py
+++ b/solution.py
@@ -17,6 +17,7 @@
 F32 = jnp.float32
 BF16 = jnp.bfloat16
 SHARE = 32
+EARLY = 3
 
 
 def two(a):
@@ -27,7 +28,7 @@
     return lax.dot_general(a, b, (((ca,), (cb,)), ((), ())), preferred_element_type=F32)
 
 
-def kernel(q, k, v, g, ld, dq, dk, dv, col, en, inner, u0s, v1s, tc, pt, ct, xu, yb, pln, zb,
+def kernel(qh, kh, vh, gh, ld, dq, dk, dv, q, k, v, g, s_in, col, en, inner, u0s, v1s, tc, pt, ct, xu, yb, pln, zb,
            sd, xd, sp, fs, dc, dx, dy, dz, wc, wx, wy, wz, s_small, r_small, s_t, r_t, s_xu, r_xu,
            s_y, r_y, s_z, r_z, s_xd, r_xd, s_f, r_f):
     iz, iy, ix, ic = (lax.axis_index(a) for a in AXES)
@@ -38,6 +39,10 @@
             return {"c": other}
         return {axis: lax.rem(lax.axis_index(axis) + i, 4)}
 
+    loads = [pltpu.make_async_copy(a, b, s_in.at[i])
+             for i, (a, b) in enumerate(((kh, k), (vh, v), (qh, q), (gh, g)))]
+    for load in loads:
+        load.start()
     barrier = pltpu.get_barrier_semaphore()
     pl.semaphore_signal(barrier, inc=1, device_id=peer("c", 1), device_id_type=MESH)
     for axis in ("x", "y", "z"):
@@ -86,9 +91,8 @@
             col[h, b] = jnp.broadcast_to(cum[h:h + 1, :], (BLOCK, BLOCK)).T
         en[b] = jnp.broadcast_to(cum[:, BLOCK - 1:BLOCK], (H, DV))
     dc[ic] = en[0] + en[1]
-
-    pl.semaphore_wait(barrier, 10)
-    c_small().start()
+    for load in loads:
+        load.wait()
 
     def products(h):
         cols = pl.ds(pl.multiple_of(h * DK, DK), DK)
@@ -107,7 +111,6 @@
         v1s[h] = parts[1][1]
         tc[h, 0] = e1 * parts[0][0] + parts[1][0]
         tc[h, 1] = e0 * parts[1][1] + parts[0][1]
-        t_copy(h).start()
 
     def chip_total(h):
         t_copy(h).wait_recv()
@@ -287,39 +290,48 @@
             wz[8 + j] = jnp.where(j < iy, jnp.exp(yf), 0.0)
             wz[12 + j] = jnp.where(j > iy, jnp.exp(yr), 0.0)
 
+    def early_loop(t, carry):
+        products(t)
+        return carry
+
+    lax.fori_loop(0, EARLY, early_loop, 0)
+    pl.semaphore_wait(barrier, 10)
+    c_small().start()
+    for t in range(EARLY):
+        t_copy(t).start()
+
     def first_loop(t, carry):
         @pl.when(t < H)
         def _():
             products(t)
-
-        @pl.when(t == 0)
+            t_copy(t).start()
+
+        @pl.when(t == EARLY)
         def _():
             core_weights()
 
-        @pl.when(t == 3)
-        def _():
-            row_weights()
-
-        @pl.when(t == 6)
-        def _():
-            plane_weights()
-
-        @pl.when(t >= 1)
-        def _():
-            chip_total(t - 1)
+        chip_total(t - EARLY)
         return carry
 
-    lax.fori_loop(0, H + 1, first_loop, 0)
-    prefix_weights()
+    lax.fori_loop(EARLY, H + EARLY, first_loop, 0)
+    row_weights()
 
     def second_loop(t, carry):
         @pl.when(t < H)
         def _():
             row_total(t)
 
+        @pl.when(t == 1)
+        def _():
+            plane_weights()
+
         @pl.when((t >= 1) & (t < H + 1))
         def _():
             plane_total(t - 1)
+
+        @pl.when(t == 2)
+        def _():
+            prefix_weights()
 
         @pl.when(t >= 2)
         def _():
@@ -364,15 +376,21 @@
 
 def body(queries, keys, values, grad_out, log_decay):
     vmem = pl.BlockSpec(memory_space=pltpu.VMEM)
-    shape = jax.ShapeDtypeStruct(queries.shape, BF16)
+    hbm = pl.BlockSpec(memory_space=pltpu.HBM)
+    shape = pltpu.VMEM(queries.shape, BF16)
     tile = pltpu.VMEM
     dma = pltpu.SemaphoreType.DMA
     return pl.pallas_call(
         kernel,
         out_shape=(shape, shape, shape),
-        in_specs=[vmem] * 5,
+        in_specs=[hbm] * 4 + [vmem],
         out_specs=(vmem, vmem, vmem),
         scratch_shapes=[
+            tile(queries.shape, BF16),
+            tile(queries.shape, BF16),
+            tile(queries.shape, BF16),
+            tile(queries.shape, BF16),
+            dma((4,)),
             tile((H, 2, BLOCK, BLOCK), F32),
             tile((2, H, DV), F32),
             tile((H, 3, 2 * BLOCK, DK), F32),
@@ -406,7 +424,7 @@
             dma((H,)), dma((H,)),
         ],
         compiler_params=pltpu.CompilerParams(
-            collective_id=0, has_side_effects=True, vmem_limit_bytes=60 * 1024 * 1024),
+            collective_id=0, has_side_effects=True, vmem_limit_bytes=50 * 1024 * 1024),
     )(queries, keys, values, grad_out, log_decay)
 
 

time: 70.4 us -> 64.5 us (0.916)
  Pallas kernels: 64.6 us -> 60.1 us
  local copies, waits for them, and re-layouts: 4.97 us -> 3.6 us
    pallas_call x1, Pallas kernels: 64.6 us -> 60.1 us  [body(): pl.pallas_call(kernel, out_shape=(shape, shape, shape), in_specs=[hbm] *...]
    unnamed x7 -> x5, local copies, waits for them, and re-layouts: 4.97 us -> 3.6 us
where the time goes in v2:
time: 64.5 us; the launch traced here: 64.3 us
  Pallas kernels  60.1 us (93%)
  local copies, waits for them, and re-layouts  3.6 us (6%)
  between operations  0.65 us (1%)
    pallas_call x1, Pallas kernels, body(): pl.pallas_call(kernel, out_shape=(shape, shape, shape), in_specs=[hbm] *...  60.1 us
    unnamed x5, local copies, waits for them, and re-layouts  3.6 us

profile of v2, /device:TPU:1, one launch (start us, length us, event | category | flops | bytes accessed | tf_op | source)
XLA Modules:
  0.0 64.3 jit_solution(7240584524776839947)
XLA Ops:
  0.6 0.0 copy-start
  0.6 0.7 %copy-done = f32[8,256]{1,0:T(8,128)S(1)} copy-done((f32[8,256]{1,0:T(8,128)S(1)}, f32[8,256]{1,0:T(8,128)}, u32[]{:S(2)}) %copy-start) | copy-done | bytes 8216
  1.3 60.1 %shard_map.76 = (bf16[256,2048]{1,0:T(8,128)(2,1)S(1)}, bf16[256,2048]{1,0:T(8,128)(2,1)S(1)}, bf16[256,2048]{1,0:T(8,128)(2,1)S(1)}) custom-call(bf16[256,2048]{1,0:T(8,128)(2,1)} %qh.1, bf16[256,2048]{1,0:T(8,128)(2,1)} %kh.1, bf16[256,2048]{1,0:T(8,128)(2,1)} %vh.1, bf16[256,2048]{1,0:T(8,128)(2,1)} %gh.1, f32[8,256]{1,0:T(8,128)S(1)} %copy-done), custom_call_target="tpu_custom_call" | custom-call | tf_op jit(solution)/shard_map/pallas_call | solution.py:383
  61.4 1.0 %copy.11 = bf16[256,2048]{1,0:T(8,128)(2,1)} copy(bf16[256,2048]{1,0:T(8,128)(2,1)S(1)} %get-tuple-element.3) | data formatting | bytes 2097152
  62.4 1.0 %copy.12 = bf16[256,2048]{1,0:T(8,128)(2,1)} copy(bf16[256,2048]{1,0:T(8,128)(2,1)S(1)} %get-tuple-element.4) | data formatting | bytes 2097152
  63.4 1.0 %copy.13 = bf16[256,2048]{1,0:T(8,128)(2,1)} copy(bf16[256,2048]{1,0:T(8,128)(2,1)S(1)} %get-tuple-element.5) | data formatting | bytes 2097152
Async XLA Ops:
  0.6 0.7 %copy-start = (f32[8,256]{1,0:T(8,128)S(1)}, f32[8,256]{1,0:T(8,128)}, u32[]{:S(2)}) copy-start(f32[8,256]{1,0:T(8,128)} %ld.1) | copy-start | bytes 24580
